TPU v7x, 256 devices: a whole 4x4x8 slice. The times are simulated.
256 devices in a mesh: var: 32 (over y, x, core), tp: 8 (over z).
Axes of the slice: x: 4, y: 4, z: 8, core: 2. Of those that a mesh axis runs over, the one named last changes fastest.
Arguments:
- tokens: bfloat16 [32768, 8192], P('var', 'tp'), may hold values from -6 to 6
- kv_weight: bfloat16 [8192, 2048], P('tp'), may hold values from -0.0625 to 0.0625
- factor_a: bfloat16 [64, 8192, 128], P('var', 'tp'), may hold values from -0.0625 to 0.0625
- factor_scale: bfloat16 [64, 128], P('var'), may hold values from 0.29882812 to 3
- factor_b: bfloat16 [64, 128, 2048], P('var', None, 'tp'), may hold values from -0.5 to 0.5
- counts: int32 [32, 64], replicated, may hold values from 0 to 64, as said below
Outputs:
- kv_out: bfloat16 [32768, 2048], P('var', 'tp')
Inputs may be any that keep to these rules, and one draw needn't show every extreme that they name: `counts`: each row sums to 1024. Owner o holds variants 2 * o to 2 * o + 1; in every row those variants together have at most 64 tokens, and in every draw one owner has exactly 64 tokens in every row.
All inputs are finite; a program needn't handle non-finite values.
Results may differ from a plain program's by a relative error of at most 0.011.
Values may be sent and summed in bfloat16 or wider, within the bound.
No kernel may reach another device: no remote copies, remote signals or barrier semaphores. Data moves between devices by JAX's collectives and lax.ppermute only.
A program may use at most 128 MiB of HBM per device.

v0:
```python
import jax
import jax.numpy as jnp
from jax import lax
from jax.sharding import PartitionSpec as P


def in_blocks(value, dim, length):
    before, after = (value.shape[:dim], value.shape[dim + 1 :])
    return jnp.moveaxis(value.reshape(*before, length, -1, *after), dim, 0)


def sum_at_owner(value, axis, dim):
    length = lax.axis_size(axis)
    parts = lax.all_to_all(in_blocks(value, dim, length), axis, 0, 0, tiled=True)
    return jnp.sum(parts.astype(jnp.float32), axis=0)


def copy_for_each(value, axis):
    copies = jnp.broadcast_to(value, (lax.axis_size(axis), *value.shape))
    return lax.all_to_all(copies, axis, split_axis=0, concat_axis=0, tiled=True)


def joined_along(parts, dim):
    parts = jnp.moveaxis(parts, 0, dim)
    lengths = parts.shape
    return parts.reshape(*lengths[:dim], lengths[dim] * lengths[dim + 1], *lengths[dim + 2 :])


def gathered_copies(value, axis, dim):
    parts = copy_for_each(value, axis)
    return joined_along(parts, dim)


def pick_table(block_counts, capacity):
    slot_ids = jnp.arange(capacity, dtype=jnp.int32)
    var_dev = block_counts.shape[1]
    bounds = jnp.cumsum(block_counts, axis=1)
    local_pick = jnp.sum(
        (slot_ids[None, :, None] >= bounds[:, None, : var_dev - 1]).astype(jnp.int32), axis=2
    )
    return (local_pick[:, :, None] == jnp.arange(var_dev, dtype=jnp.int32)[None, None, :]).astype(
        jnp.float32
    )


def rank_project(blocks, picker, factor_in, equation):
    products = jnp.einsum(equation, blocks, factor_in, preferred_element_type=jnp.float32)
    return jnp.sum(products * picker[..., None], axis=2)


def expand_rank(rank_part, picker, scale_table, factor_out, equation):
    rank_share = sum_at_owner(rank_part.astype(jnp.bfloat16), "tp", 1)
    share_rows = rank_share.shape[1]
    offset = lax.axis_index("tp") * share_rows
    pick_share = lax.dynamic_slice_in_dim(picker, offset, share_rows, 1)
    scaled_share = (rank_share * jnp.sum(pick_share[..., None] * scale_table, axis=2)).astype(
        jnp.bfloat16
    )
    scaled = gathered_copies(scaled_share, "tp", 1)
    outputs = jnp.einsum(equation, scaled, factor_out, preferred_element_type=jnp.float32)
    return jnp.sum(outputs * picker[..., None], axis=2).astype(jnp.bfloat16)


def body(tokens, kv_weight, factor_a, factor_scale, factor_b, counts):
    var_count = lax.axis_size("var")
    owner_index = lax.axis_index("var")
    tok_rows = tokens.shape[0]
    var_dev = factor_a.shape[0]
    capacity = 2 * tok_rows // var_count
    partial_value = jnp.dot(tokens, kv_weight, preferred_element_type=jnp.float32)
    base_part = lax.psum_scatter(
        partial_value.astype(jnp.bfloat16), "tp", scatter_dimension=1, tiled=True
    ).astype(jnp.float32)
    own_counts = lax.dynamic_index_in_dim(counts, owner_index, 0, keepdims=False)
    owner_counts = own_counts.reshape(var_count, var_dev)
    starts = jnp.cumsum(own_counts) - own_counts
    first_rows = starts.reshape(var_count, var_dev)[:, 0]
    slot_ids = jnp.arange(capacity, dtype=jnp.int32)
    inside = slot_ids[None, :] < jnp.sum(owner_counts, axis=1)[:, None]
    row_index = jnp.clip(first_rows[:, None] + slot_ids[None, :], 0, tok_rows - 1)
    outgoing = jnp.where(inside[:, :, None], tokens[row_index], jnp.zeros((), tokens.dtype))
    every_in, every_out, every_scale = (
        lax.all_gather(factor_a, "var", axis=0, tiled=True),
        lax.all_gather(factor_b, "var", axis=0, tiled=True),
        lax.all_gather(factor_scale, "var", axis=0, tiled=True),
    )
    picker = pick_table(owner_counts, capacity)
    factor_in = every_in.reshape(var_count, var_dev, every_in.shape[1], every_in.shape[2])
    factor_out = every_out.reshape(var_count, var_dev, every_out.shape[1], every_out.shape[2])
    scale_table = every_scale.astype(jnp.float32).reshape(
        var_count, 1, var_dev, every_scale.shape[1]
    )
    rank_part = rank_project(outgoing, picker, factor_in, "ocd,ovdr->ocvr")
    delta_blocks = expand_rank(rank_part, picker, scale_table, factor_out, "ocr,ovrk->ocvk")
    ends_at = jnp.cumsum(own_counts)
    position = jnp.arange(tok_rows, dtype=jnp.int32)
    variant = jnp.sum((ends_at[None, :] <= position[:, None]).astype(jnp.int32), axis=1)
    owner_of = variant // var_dev
    owner_hot = owner_of[:, None] == jnp.arange(var_count, dtype=jnp.int32)[None, :]
    owner_first = jnp.sum(jnp.where(owner_hot, first_rows[None, :], 0), axis=1)
    flat_index = owner_of * capacity + position - owner_first
    delta_rows = delta_blocks.reshape(var_count * capacity, delta_blocks.shape[2])[flat_index]
    return (base_part + delta_rows.astype(jnp.float32)).astype(jnp.bfloat16)


def solution(mesh):
    return jax.shard_map(
        body,
        mesh=mesh,
        in_specs=(
            P("var", "tp"),
            P("tp", None),
            P("var", "tp", None),
            P("var", None),
            P("var", None, "tp"),
            P(),
        ),
        out_specs=P("var", "tp"),
        check_vma=False,
    )
```

profile of v0, /device:TPU:1, one launch (start us, length us, event | category | flops | bytes accessed | tf_op | source)
XLA Modules:
  0.0 176.4 jit_solution(6263837088870079892)
XLA Ops:
  7.4 0.7 all-gather.4.cloned.1.call-update
  8.1 0.7 all-gather.6.cloned.1.call-update
  9.0 8.2 %convolution_convert_fusion = bf16[1024,2048]{1,0:T(8,128)(2,1)} fusion(bf16[1024,1024]{1,0:T(8,128)(2,1)S(1)} %copy-done, bf16[1024,2048]{1,0:T(8,128)(2,1)} %param.7), kind=kOutput, calls=%fused_computation.7 | convolution fusion | flops 4297064448 | bytes 10485760 | tf_op jit(solution)/shard_map/dot_general | solution.py:70
  17.2 0.7 fusion.13
  17.9 0.1 reshape.219
  18.0 0.2 reduce_window_sum.19
  18.2 0.1 reduce_sum.71
  18.3 0.1 copy.18
  18.4 0.1 reduce-window.4
  18.5 0.1 reduce.1
  18.6 0.1 reshape.221
  18.7 0.1 fusion.9
  18.9 0.1 reshape.228
  19.0 9.7 %gather_fusion = bf16[2048,1024]{1,0:T(8,128)(2,1)} fusion(bf16[1024,1024]{1,0:T(8,128)(2,1)S(1)} %copy-done, s32[2048]{0:T(1024)S(1)} %broadcast_clamp_fusion), kind=kCustom, calls=%fused_computation | custom fusion | bytes 8396800 | tf_op jit(solution)/shard_map/gather | solution.py:81
  28.7 0.1 slice_reduce_fusion
  29.0 63.6 %all-gather.4.cloned.1.call-done = bf16[64,1024,128]{2,1,0:T(8,128)(2,1)} async-done(((bf16[2,1024,128]{2,1,0:T(8,128)(2,1)}), bf16[64,1024,128]{2,1,0:T(8,128)(2,1)}) %all-gather.4.cloned.1.call-update) | async-done | bytes 16777232 | tf_op jit(solution)/shard_map/all_gather | solution.py:83
  92.6 10.2 %multiply_reduce_fusion.1 = bf16[32,64,128]{2,1,0:T(8,128)(2,1)S(1)} fusion(f32[32,64,2]{1,2,0:T(2,128)S(1)} %compare_convert_fusion, bf16[32,2,1024,128]{3,2,1,0:T(8,128)(2,1)} %bitcast.47, bf16[32,64,1024]{2,1,0:T(8,128)(2,1)} %bitcast.40, pred[32,64]{1,0:T(8,128)(4,1)S(1)} %iota_compare_fusion.3), kind=kOutput, calls=%fused_computation.8 | convolution fusion | flops 1076625408 | bytes 21514240 | tf_op jit(solution)/shard_map/ocd,ovdr->ocvr/dot_general | solution.py:47
  102.8 0.9 copy.19
  103.7 6.7 %all-to-all-start = ((bf16[8,32,8,128]{3,2,1,0:T(8,128)(2,1)}), bf16[8,32,8,128]{3,2,1,0:T(8,128)(2,1)S(1)}, u32[]{:S(2)}, u32[]{:S(2)}) async-start(bf16[8,32,8,128]{3,2,1,0:T(8,128)(2,1)} %copy.19), calls=%async_computation.1 | async-start | bytes 1048576 | tf_op jit(solution)/shard_map/all_to_all | solution.py:14
  110.4 21.2 %all-gather = bf16[32,2,128]{2,1,0:T(2,128)(2,1)S(1)} all-gather(bf16[1,2,128]{2,1,0:T(2,128)(2,1)S(1)} %bitcast.46), channel_id=1, replica_groups=mesh['var'=32,'tp'=8] {'var'}, dimensions={0}, use_global_device_ids=true | all-gather | bytes 16896 | tf_op jit(solution)/shard_map/all_gather | solution.py:85
  131.7 0.1 constant_dynamic-slice_fusion
  131.8 0.1 multiply_reduce_fusion.2
  132.0 0.9 broadcast_in_dim.24
  132.9 6.9 %all-to-all-start.1 = ((bf16[8,32,8,128]{3,2,1,0:T(8,128)(2,1)}), bf16[8,32,8,128]{3,2,1,0:T(8,128)(2,1)S(1)}, u32[]{:S(2)}, u32[]{:S(2)}) async-start(bf16[8,32,8,128]{3,2,1,0:T(8,128)(2,1)} %broadcast_in_dim.24), calls=%async_computation.2 | async-start | bytes 1048576 | tf_op jit(solution)/shard_map/all_to_all | solution.py:20
  139.8 0.1 convert_reduce_fusion.1
  139.9 0.1 select_reduce_fusion
  140.1 5.7 %all-gather.6.cloned.1.call-done = bf16[64,128,256]{2,1,0:T(8,128)(2,1)} async-done(((bf16[2,128,256]{2,1,0:T(8,128)(2,1)}), bf16[64,128,256]{2,1,0:T(8,128)(2,1)}) %all-gather.6.cloned.1.call-update) | async-done | bytes 4194320 | tf_op jit(solution)/shard_map/all_gather | solution.py:84
  145.7 12.0 %all-to-all-done.1 = bf16[8,32,8,128]{3,2,1,0:T(8,128)(2,1)S(1)} async-done(((bf16[8,32,8,128]{3,2,1,0:T(8,128)(2,1)}), bf16[8,32,8,128]{3,2,1,0:T(8,128)(2,1)S(1)}, u32[]{:S(2)}, u32[]{:S(2)}) %all-to-all-start.1) | async-done | bytes 524320 | tf_op jit(solution)/shard_map/all_to_all | solution.py:20
  157.8 0.8 copy-done.1
  158.6 3.3 %multiply_reduce_fusion = bf16[32,64,256]{2,1,0:T(8,128)(2,1)S(1)} fusion(bf16[32,2,128,256]{3,2,1,0:T(8,128)(2,1)} %bitcast.41, f32[32,64,2]{1,2,0:T(2,128)S(1)} %compare_convert_fusion, bf16[8,32,8,128]{3,2,1,0:T(8,128)(2,1)} %copy-done.1), kind=kOutput, calls=%fused_computation.4 | convolution fusion | flops 270008320 | bytes 5783552 | tf_op jit(solution)/shard_map/ocr,ovrk->ocvk/dot_general | solution.py:60
  161.9 5.0 %gather_fusion.1 = bf16[1024,256]{1,0:T(8,128)(2,1)} fusion(bf16[2048,256]{1,0:T(8,128)(2,1)S(1)} %bitcast.39, s32[1024]{0:T(1024)S(1)} %broadcast_clamp_fusion.1), kind=kCustom, calls=%fused_computation.1 | custom fusion | bytes 1052672 | tf_op jit(solution)/shard_map/gather | solution.py:102
  166.8 2.1 %add_convert_fusion = bf16[1024,256]{1,0:T(8,128)(2,1)} fusion(bf16[1024,256]{1,0:T(8,128)(2,1)} %gather_fusion.1, bf16[1024,256]{1,0:T(8,128)(2,1)} %reduce-scatter.2.cloned.1.call-done), kind=kLoop, calls=%fused_computation.10 | loop fusion | flops 1048576 | bytes 1572864 | tf_op jit(solution)/shard_map/convert_element_type | solution.py:103
  (22 shorter events, 0.6 us)
Async XLA Ops:
  7.4 1.6 copy-start
  7.4 85.2 %all-gather.4.cloned.1.call-start = ((), (), s32[]{:S(2)}) async-start(), calls=%async_computation.4 | async-start | bytes 17301504 | tf_op jit(solution)/shard_map/all_gather | solution.py:83
  8.1 137.6 %all-gather.6.cloned.1.call-start = ((), (), s32[]{:S(2)}) async-start(), calls=%async_computation.5 | async-start | bytes 4325376 | tf_op jit(solution)/shard_map/all_gather | solution.py:84
  8.8 158.0 %reduce-scatter.2.cloned.1.call-start = ((), (), s32[]{:S(2)}) async-start(), calls=%async_computation.3 | async-start | bytes 4718592 | tf_op jit(solution)/shard_map/reduce_scatter | solution.py:71
  92.6 17.9 %copy-start.2 = (bf16[2,128]{1,0:T(2,128)(2,1)S(1)}, bf16[2,128]{1,0:T(2,128)(2,1)}, u32[]{:S(2)}) copy-start(bf16[2,128]{1,0:T(2,128)(2,1)} %param.9) | copy-start | bytes 1540
  103.7 28.2 %all-to-all-start = ((bf16[8,32,8,128]{3,2,1,0:T(8,128)(2,1)}), bf16[8,32,8,128]{3,2,1,0:T(8,128)(2,1)S(1)}, u32[]{:S(2)}, u32[]{:S(2)}) async-start(bf16[8,32,8,128]{3,2,1,0:T(8,128)(2,1)} %copy.19), calls=%async_computation.1 | async-start | bytes 1048576 | tf_op jit(solution)/shard_map/all_to_all | solution.py:14
  132.9 24.9 %all-to-all-start.1 = ((bf16[8,32,8,128]{3,2,1,0:T(8,128)(2,1)}), bf16[8,32,8,128]{3,2,1,0:T(8,128)(2,1)S(1)}, u32[]{:S(2)}, u32[]{:S(2)}) async-start(bf16[8,32,8,128]{3,2,1,0:T(8,128)(2,1)} %broadcast_in_dim.24), calls=%async_computation.2 | async-start | bytes 1048576 | tf_op jit(solution)/shard_map/all_to_all | solution.py:20
  157.8 0.8 copy-start.1
Sparse Core Ops, SparseCore 0:
  10.7 81.7 all-gather.3
  95.1 50.5 all-gather.5
Sparse Core Ops, SparseCore 1:
  17.3 59.0 reduce-scatter.1
where the time goes:
time: 177 us; the launch traced here: 176 us
  waiting for transfers between devices  82.7 us (47%)
  matrix products  21.7 us (12%)
  blocking collectives  21.2 us (12%)
  local copies, waits for them, and re-layouts  18.6 us (11%)
  between operations  15 us (8%)
  starting transfers between devices  13.7 us (8%)
  other arithmetic  3.44 us (2%)
    all_gather x1, waiting for transfers between devices, body(): lax.all_gather(factor_a, 'var', axis=0, tiled=True)  63.6 us
    all_gather x1, blocking collectives, body(): lax.all_gather(factor_scale, 'var', axis=0, tiled=True)  21.2 us
    all_to_all x1, waiting for transfers between devices, copy_for_each(): return lax.all_to_all(copies, axis, split_axis=0, concat_axis=0, tiled=True)  12 us
    dot_general x1, matrix products, rank_project(): jnp.einsum(equation, blocks, factor_in, preferred_element_type=jnp.float32)  10.2 us
    gather x1, local copies, waits for them, and re-layouts, body(): tokens[row_index]  9.7 us
    dot_general x1, matrix products, body(): jnp.dot(tokens, kv_weight, preferred_element_type=jnp.float32)  8.22 us
    all_to_all x1, starting transfers between devices, copy_for_each(): return lax.all_to_all(copies, axis, split_axis=0, concat_axis=0, tiled=True)  6.89 us
    all_to_all x1, starting transfers between devices, sum_at_owner(): lax.all_to_all(in_blocks(value, dim, length), axis, 0, 0, tiled=True)  6.73 us
  transfers between devices with their start and end apart: 5, of which 3 were waited for; matrix products, arithmetic and copies ran while one was open for 23% of the time, Pallas kernels for 0%

commit v1 on v0

--- a/solution.py
+++ b/solution.py
@@ -2,6 +2,11 @@
 import jax.numpy as jnp
 from jax import lax
 from jax.sharding import PartitionSpec as P
+
+
+def gather_by_exchange(value, axis, dim):
+    copies = jnp.concatenate([value] * lax.axis_size(axis), axis=dim)
+    return lax.all_to_all(copies, axis, dim, dim, tiled=True)
 
 
 def in_blocks(value, dim, length):
@@ -82,7 +87,7 @@
     every_in, every_out, every_scale = (
         lax.all_gather(factor_a, "var", axis=0, tiled=True),
         lax.all_gather(factor_b, "var", axis=0, tiled=True),
-        lax.all_gather(factor_scale, "var", axis=0, tiled=True),
+        gather_by_exchange(factor_scale, "var", 0),
     )
     picker = pick_table(owner_counts, capacity)
     factor_in = every_in.reshape(var_count, var_dev, every_in.shape[1], every_in.shape[2])

time: 177 us -> 170 us (0.960)
  blocking collectives: 21.2 us -> 0 us
  local copies, waits for them, and re-layouts: 18.6 us -> 24 us
  starting transfers between devices: 13.7 us -> 18.9 us
  waiting for transfers between devices: 82.7 us -> 86.4 us
    all_gather x1 -> x0, blocking collectives: 21.2 us -> none  [body(): lax.all_gather(factor_scale, 'var', axis=0, tiled=True)]
    all_to_all x1, waiting for transfers between devices: 0.01 us -> 17.7 us  [sum_at_owner(): lax.all_to_all(in_blocks(value, dim, length), axis, 0, 0, tiled=True)]
    all_gather x1, waiting for transfers between devices: 63.6 us -> 49.7 us  [body(): lax.all_gather(factor_a, 'var', axis=0, tiled=True)]
    all_to_all x0 -> x1, starting transfers between devices: none -> 8.58 us  [gather_by_exchange(): return lax.all_to_all(copies, axis, dim, dim, tiled=True)]
    all_to_all x1, waiting for transfers between devices: 12 us -> 4.98 us  [copy_for_each(): return lax.all_to_all(copies, axis, split_axis=0, concat_axis=0, tiled=True)]
    all_gather x1, waiting for transfers between devices: 5.66 us -> 12.6 us  [body(): lax.all_gather(factor_b, 'var', axis=0, tiled=True)]
    concatenate x0 -> x1, local copies, waits for them, and re-layouts: none -> 4.77 us  [gather_by_exchange(): copies = jnp.concatenate([value] * lax.axis_size(axis), axis=dim)]
    all_to_all x1, starting transfers between devices: 6.89 us -> 3.49 us  [copy_for_each(): return lax.all_to_all(copies, axis, split_axis=0, concat_axis=0, tiled=True)]
  transfers between devices with their start and end apart: 5 -> 6, of which waited for: 3 -> 4; matrix products, arithmetic and copies ran while one was open for 23% -> 27% of each run, Pallas kernels for 0% -> 0%
where the time goes in v1:
time: 170 us; the launch traced here: 169 us
  waiting for transfers between devices  86.4 us (51%)
  local copies, waits for them, and re-layouts  24 us (14%)
  matrix products  21.7 us (13%)
  starting transfers between devices  18.9 us (11%)
  between operations  15 us (9%)
  other arithmetic  3.44 us (2%)
    all_gather x1, waiting for transfers between devices, body(): lax.all_gather(factor_a, 'var', axis=0, tiled=True)  49.7 us
    all_to_all x1, waiting for transfers between devices, sum_at_owner(): lax.all_to_all(in_blocks(value, dim, length), axis, 0, 0, tiled=True)  17.7 us
    all_gather x1, waiting for transfers between devices, body(): lax.all_gather(factor_b, 'var', axis=0, tiled=True)  12.6 us
    dot_general x1, matrix products, rank_project(): jnp.einsum(equation, blocks, factor_in, preferred_element_type=jnp.float32)  10.2 us
    gather x1, local copies, waits for them, and re-layouts, body(): tokens[row_index]  9.7 us
    all_to_all x1, starting transfers between devices, gather_by_exchange(): return lax.all_to_all(copies, axis, dim, dim, tiled=True)  8.58 us
    dot_general x1, matrix products, body(): jnp.dot(tokens, kv_weight, preferred_element_type=jnp.float32)  8.22 us
    all_to_all x1, starting transfers between devices, sum_at_owner(): lax.all_to_all(in_blocks(value, dim, length), axis, 0, 0, tiled=True)  6.73 us
  transfers between devices with their start and end apart: 6, of which 4 were waited for; matrix products, arithmetic and copies ran while one was open for 27% of the time, Pallas kernels for 0%

profile of v1, /device:TPU:1, one launch (start us, length us, event | category | flops | bytes accessed | tf_op | source)
XLA Modules:
  0.0 169.4 jit_solution(7242241947404643095)
XLA Ops:
  7.4 0.7 all-gather.3.cloned.1.call-update
  8.1 0.7 all-gather.5.cloned.1.call-update
  9.0 8.2 %convolution_convert_fusion = bf16[1024,2048]{1,0:T(8,128)(2,1)} fusion(bf16[1024,1024]{1,0:T(8,128)(2,1)S(1)} %copy-done, bf16[1024,2048]{1,0:T(8,128)(2,1)} %param.7), kind=kOutput, calls=%fused_computation.7 | convolution fusion | flops 4297064448 | bytes 10485760 | tf_op jit(solution)/shard_map/dot_general | solution.py:75
  17.2 0.6 copy-done.2
  17.8 4.8 %concatenate.3 = bf16[64,128]{1,0:T(8,128)(2,1)} concatenate(bf16[2,128]{1,0:T(2,128)(2,1)S(1)} %copy-done.2, bf16[2,128]{1,0:T(2,128)(2,1)S(1)} %copy-done.2, bf16[2,128]{1,0:T(2,128)(2,1)S(1)} %copy-done.2, bf16[2,128]{1,0:T(2,128)(2,1)S(1)} %copy-done.2, bf16[2,128]{1,0:T(2,128)(2,1)S(1)} %copy-done.2, bf16[2,128]{1,0:T(2,128)(2,1)S(1)} %copy-done.2, ...), dimensions={0} | concatenate | bytes 32768 | tf_op jit(solution)/shard_map/concatenate | solution.py:8
  22.6 8.6 %all-to-all-start.1 = ((bf16[32,2,128]{2,1,0:T(2,128)(2,1)}), bf16[32,2,128]{2,1,0:T(2,128)(2,1)S(1)}, u32[]{:S(2)}, u32[]{:S(2)}) async-start(bf16[32,2,128]{2,1,0:T(2,128)(2,1)} %bitcast.7), calls=%async_computation.2 | async-start | bytes 32768 | tf_op jit(solution)/shard_map/all_to_all | solution.py:9
  31.2 0.7 fusion.13
  31.9 0.1 reshape.223
  32.0 0.2 reduce_window_sum.19
  32.2 0.1 reduce_sum.71
  32.3 0.1 copy.18
  32.4 0.1 reduce-window.4
  32.5 0.1 reduce.1
  32.6 0.1 reshape.225
  32.7 0.1 fusion.9
  33.0 9.7 %gather_fusion = bf16[2048,1024]{1,0:T(8,128)(2,1)} fusion(bf16[1024,1024]{1,0:T(8,128)(2,1)S(1)} %copy-done, s32[2048]{0:T(1024)S(1)} %broadcast_clamp_fusion), kind=kCustom, calls=%fused_computation | custom fusion | bytes 8396800 | tf_op jit(solution)/shard_map/gather | solution.py:86
  42.7 0.1 slice_reduce_fusion
  43.0 49.7 %all-gather.3.cloned.1.call-done = bf16[64,1024,128]{2,1,0:T(8,128)(2,1)} async-done(((bf16[2,1024,128]{2,1,0:T(8,128)(2,1)}), bf16[64,1024,128]{2,1,0:T(8,128)(2,1)}) %all-gather.3.cloned.1.call-update) | async-done | bytes 16777232 | tf_op jit(solution)/shard_map/all_gather | solution.py:88
  92.6 10.2 %multiply_reduce_fusion.1 = bf16[32,64,128]{2,1,0:T(8,128)(2,1)S(1)} fusion(f32[32,64,2]{1,2,0:T(2,128)S(1)} %compare_convert_fusion, bf16[32,2,1024,128]{3,2,1,0:T(8,128)(2,1)} %bitcast.46, bf16[32,64,1024]{2,1,0:T(8,128)(2,1)} %bitcast.40, pred[32,64]{1,0:T(8,128)(4,1)S(1)} %iota_compare_fusion.3), kind=kOutput, calls=%fused_computation.8 | convolution fusion | flops 1076625408 | bytes 21514240 | tf_op jit(solution)/shard_map/ocd,ovdr->ocvr/dot_general | solution.py:52
  102.9 0.9 copy.19
  103.7 6.7 %all-to-all-start = ((bf16[8,32,8,128]{3,2,1,0:T(8,128)(2,1)}), bf16[8,32,8,128]{3,2,1,0:T(8,128)(2,1)S(1)}, u32[]{:S(2)}, u32[]{:S(2)}) async-start(bf16[8,32,8,128]{3,2,1,0:T(8,128)(2,1)} %copy.19), calls=%async_computation.1 | async-start | bytes 1048576 | tf_op jit(solution)/shard_map/all_to_all | solution.py:19
  110.6 0.1 multiply_reduce_fusion.2
  110.7 17.7 %all-to-all-done = bf16[8,32,8,128]{3,2,1,0:T(8,128)(2,1)S(1)} async-done(((bf16[8,32,8,128]{3,2,1,0:T(8,128)(2,1)}), bf16[8,32,8,128]{3,2,1,0:T(8,128)(2,1)S(1)}, u32[]{:S(2)}, u32[]{:S(2)}) %all-to-all-start) | async-done | bytes 524320 | tf_op jit(solution)/shard_map/all_to_all | solution.py:19
  128.5 0.9 broadcast_in_dim.24
  129.4 3.5 %all-to-all-start.2 = ((bf16[8,32,8,128]{3,2,1,0:T(8,128)(2,1)}), bf16[8,32,8,128]{3,2,1,0:T(8,128)(2,1)S(1)}, u32[]{:S(2)}, u32[]{:S(2)}) async-start(bf16[8,32,8,128]{3,2,1,0:T(8,128)(2,1)} %broadcast_in_dim.24), calls=%async_computation.3 | async-start | bytes 1048576 | tf_op jit(solution)/shard_map/all_to_all | solution.py:25
  132.9 0.1 convert_reduce_fusion.1
  133.2 12.6 %all-gather.5.cloned.1.call-done = bf16[64,128,256]{2,1,0:T(8,128)(2,1)} async-done(((bf16[2,128,256]{2,1,0:T(8,128)(2,1)}), bf16[64,128,256]{2,1,0:T(8,128)(2,1)}) %all-gather.5.cloned.1.call-update) | async-done | bytes 4194320 | tf_op jit(solution)/shard_map/all_gather | solution.py:89
  145.8 5.0 %all-to-all-done.2 = bf16[8,32,8,128]{3,2,1,0:T(8,128)(2,1)S(1)} async-done(((bf16[8,32,8,128]{3,2,1,0:T(8,128)(2,1)}), bf16[8,32,8,128]{3,2,1,0:T(8,128)(2,1)S(1)}, u32[]{:S(2)}, u32[]{:S(2)}) %all-to-all-start.2) | async-done | bytes 524320 | tf_op jit(solution)/shard_map/all_to_all | solution.py:25
  150.8 0.8 copy-done.1
  151.6 3.3 %multiply_reduce_fusion = bf16[32,64,256]{2,1,0:T(8,128)(2,1)S(1)} fusion(bf16[32,2,128,256]{3,2,1,0:T(8,128)(2,1)} %bitcast.41, f32[32,64,2]{1,2,0:T(2,128)S(1)} %compare_convert_fusion, bf16[8,32,8,128]{3,2,1,0:T(8,128)(2,1)} %copy-done.1), kind=kOutput, calls=%fused_computation.4 | convolution fusion | flops 270008320 | bytes 5783552 | tf_op jit(solution)/shard_map/ocr,ovrk->ocvk/dot_general | solution.py:65
  154.9 5.0 %gather_fusion.1 = bf16[1024,256]{1,0:T(8,128)(2,1)} fusion(bf16[2048,256]{1,0:T(8,128)(2,1)S(1)} %bitcast.39, s32[1024]{0:T(1024)S(1)} %broadcast_clamp_fusion.1), kind=kCustom, calls=%fused_computation.1 | custom fusion | bytes 1052672 | tf_op jit(solution)/shard_map/gather | solution.py:107
  159.8 2.1 %add_convert_fusion = bf16[1024,256]{1,0:T(8,128)(2,1)} fusion(bf16[1024,256]{1,0:T(8,128)(2,1)} %gather_fusion.1, bf16[1024,256]{1,0:T(8,128)(2,1)} %reduce-scatter.2.cloned.1.call-done), kind=kLoop, calls=%fused_computation.10 | loop fusion | flops 1048576 | bytes 1572864 | tf_op jit(solution)/shard_map/convert_element_type | solution.py:108
  (24 shorter events, 0.8 us)
Async XLA Ops:
  7.4 1.6 copy-start
  7.4 85.3 %all-gather.3.cloned.1.call-start = ((), (), s32[]{:S(2)}) async-start(), calls=%async_computation.5 | async-start | bytes 17301504 | tf_op jit(solution)/shard_map/all_gather | solution.py:88
  8.1 137.7 %all-gather.5.cloned.1.call-start = ((), (), s32[]{:S(2)}) async-start(), calls=%async_computation.6 | async-start | bytes 4325376 | tf_op jit(solution)/shard_map/all_gather | solution.py:89
  8.8 151.0 %reduce-scatter.2.cloned.1.call-start = ((), (), s32[]{:S(2)}) async-start(), calls=%async_computation.4 | async-start | bytes 4718592 | tf_op jit(solution)/shard_map/reduce_scatter | solution.py:76
  17.2 0.7 copy-start.2
  22.6 81.1 %all-to-all-start.1 = ((bf16[32,2,128]{2,1,0:T(2,128)(2,1)}), bf16[32,2,128]{2,1,0:T(2,128)(2,1)S(1)}, u32[]{:S(2)}, u32[]{:S(2)}) async-start(bf16[32,2,128]{2,1,0:T(2,128)(2,1)} %bitcast.7), calls=%async_computation.2 | async-start | bytes 32768 | tf_op jit(solution)/shard_map/all_to_all | solution.py:9
  103.7 24.7 %all-to-all-start = ((bf16[8,32,8,128]{3,2,1,0:T(8,128)(2,1)}), bf16[8,32,8,128]{3,2,1,0:T(8,128)(2,1)S(1)}, u32[]{:S(2)}, u32[]{:S(2)}) async-start(bf16[8,32,8,128]{3,2,1,0:T(8,128)(2,1)} %copy.19), calls=%async_computation.1 | async-start | bytes 1048576 | tf_op jit(solution)/shard_map/all_to_all | solution.py:19
  129.4 21.4 %all-to-all-start.2 = ((bf16[8,32,8,128]{3,2,1,0:T(8,128)(2,1)}), bf16[8,32,8,128]{3,2,1,0:T(8,128)(2,1)S(1)}, u32[]{:S(2)}, u32[]{:S(2)}) async-start(bf16[8,32,8,128]{3,2,1,0:T(8,128)(2,1)} %broadcast_in_dim.24), calls=%async_computation.3 | async-start | bytes 1048576 | tf_op jit(solution)/shard_map/all_to_all | solution.py:25
  150.8 0.8 copy-start.1
Sparse Core Ops, SparseCore 0:
  10.7 81.8 all-gather.2
  95.2 50.5 all-gather.4
Sparse Core Ops, SparseCore 1:
  17.3 58.9 reduce-scatter.1
